TPU v7x, 32 devices: a whole 2x2x4 slice. The times are simulated.
32 devices in a mesh: tm: 4 (over z), batch: 4 (over x, core), width: 2 (over y).
Axes of the slice: x: 2, y: 2, z: 4, core: 2. Of those that a mesh axis runs over, the one named last changes fastest.
Arguments:
- moves: int32 [8, 1024], P('batch', 'tm'), may hold values from 0 to 361
- lengths: int32 [8], P('batch'), may hold values from 1 to 1024
- outcomes: int32 [8], P('batch'), may hold values from -1 to 1
- embedded: bfloat16 [8, 1024, 2048], P('batch', 'tm', 'width'), may hold values from -6 to 6
- w_branches: bfloat16 [4, 2048, 2048], P(None, ('tm', 'batch'), 'width'), may hold values from -0.125 to 0.125
- conv_w: float32 [4, 2048], P(None, 'width'), may hold values from -3 to 3
- gate_bias: float32 [2, 2048], P(None, 'width'), may hold values from -4 to 4
- rates: float32 [2048], P('width'), may hold values from 0.001 to 0.105
- w_down: bfloat16 [2048, 2048], P(('tm', 'batch'), 'width'), may hold values from -0.125 to 0.125
- w_policy: bfloat16 [2048, 362], P('width'), may hold values from -12 to 12
- w_value: bfloat16 [2048], P('width'), may hold values from -0.125 to 0.125
Outputs:
- position_loss: float32 [8, 1024], P('batch', 'tm')
- value: float32 [8, 1024], P('batch', 'tm')
All inputs are finite; a program needn't handle non-finite values.
Results may differ from a plain program's by a relative error of at most 0.0033.
Values may be sent and summed in bfloat16 or wider, within the bound.
A program may use at most 128 MiB of HBM per device.

v0:
```python
import jax
import jax.numpy as jnp
from jax import lax
from jax.experimental import pallas as pl
from jax.experimental.pallas import tpu as pltpu
from jax.sharding import PartitionSpec as P

KERNEL = 4
SUB = 8
MESH = pl.DeviceIdType.MESH
STREAMS = tuple(range(6))
LAG = 2


def swap(value, axis):
    n = lax.axis_size(axis)
    return lax.ppermute(value, axis, [(i, n - 1 - i) for i in range(n)])


def interleave(x):
    games, steps = x.shape[:2]
    return jnp.swapaxes(x.reshape(games, SUB, steps // SUB, *x.shape[2:]), 1, 2).reshape(x.shape)


def restore(x):
    games, steps = x.shape[:2]
    return jnp.swapaxes(x.reshape(games, steps // SUB, SUB, *x.shape[2:]), 1, 2).reshape(x.shape)


def both(own, other, axis, dim):
    first = lax.axis_index(axis) == 0
    return jnp.concatenate([jnp.where(first, own, other), jnp.where(first, other, own)], dim)


def core_kernel(
    emb, wb, wd, tail, conv_w, bias, rates,
    resid,
    w_all, acc, tails, halo, carry_s, wd_all, feat, ends, state, mixed, out_buf, in_buf, kept,
    loc, feat_s, feat_r, tail_s, tail_r, ring_s, ring_r, peer_s, peer_r, ends_s, ends_r, out_s, out_r,
):
    z, b, y = lax.axis_index("tm"), lax.axis_index("batch"), lax.axis_index("width")
    zn, bn, yn = lax.axis_size("tm"), lax.axis_size("batch"), lax.axis_size("width")
    x, core = b // 2, b % 2
    n = zn * (bn // 2)
    rows, chans = wd.shape
    count, half = emb.shape
    games = ends.shape[1]
    width_cut = chans // 2

    def spot(r):
        cx = r // zn
        cz = r % zn
        return cz + (cx % 2) * (zn - 1 - 2 * cz), cx

    r = x * zn + z + (x % 2) * (zn - 1 - 2 * z)

    def at(place, c=core, w=y):
        return {"tm": place[0], "batch": place[1] * 2 + c, "width": w}

    ahead, behind = at(spot((r + 1) % n)), at(spot((r + n - 1) % n))
    peer = at((z, x), 1 - core)
    partner = at((z, x), core, yn - 1 - y)
    later, earlier = ((z + 1) % zn, x), ((z + zn - 1) % zn, x)
    tail_to = [at(later), at(later, core, yn - 1 - y)]
    greet = [ahead, behind, peer, partner] + tail_to + [at(earlier), at(earlier, core, yn - 1 - y)]
    greet += [at(((z + d) % zn, x)) for d in range(2, zn - 1)]

    def first_row(chip):
        cz, cx = spot(chip)
        return (cz * bn + cx * 2) * rows

    own = first_row(r) + core * rows
    own = pl.multiple_of(own, rows)
    local = [
        pltpu.make_async_copy(wb, w_all.at[:, pl.ds(own, rows), :], loc.at[0]),
        pltpu.make_async_copy(wd, wd_all.at[pl.ds(own, rows), :], loc.at[1]),
        pltpu.make_async_copy(emb, feat.at[y], loc.at[2]),
        pltpu.make_async_copy(tail, tails.at[2], loc.at[3]),
    ]
    for copy in local:
        copy.start()
    barrier = pltpu.get_barrier_semaphore()
    for device in greet:
        pl.semaphore_signal(barrier, inc=1, device_id=device, device_id_type=MESH)
    pl.semaphore_wait(barrier, len(greet))
    for copy in local:
        copy.wait()

    def remote(src, dst, send, recv, device):
        return pltpu.make_async_remote_copy(
            src_ref=src, dst_ref=dst, send_sem=send, recv_sem=recv, device_id=device, device_id_type=MESH
        )

    def forward(s):
        return s in (0, 1, 4)

    def chip_of(s, t):
        return (r + n - t) % n if forward(s) else (r + t) % n

    def piece(s, chip, c):
        at_row = pl.ds(pl.multiple_of(first_row(chip) + c * rows, rows), rows)
        if s < 4:
            return w_all.at[s, at_row, :]
        return wd_all.at[at_row, pl.ds((s - 4) * width_cut, width_cut)]

    def hop(s, t):
        ref = piece(s, chip_of(s, t - 1), core)
        return remote(ref, ref, ring_s.at[s, t], ring_r.at[s, t], ahead if forward(s) else behind)

    def landed(s, t):
        ref = piece(s, chip_of(s, t), core)
        return remote(ref, ref, ring_s.at[s, t], ring_r.at[s, t], ahead if forward(s) else behind)

    def share(s, t):
        ref = piece(s, chip_of(s, t), core)
        return remote(ref, ref, peer_s.at[s, t], peer_r.at[s, t], peer)

    def shared(s, t):
        ref = piece(s, chip_of(s, t), 1 - core)
        return remote(ref, ref, peer_s.at[s, t], peer_r.at[s, t], peer)

    for s in STREAMS[:4]:
        hop(s, 1).start()
    swap_feat = remote(feat.at[y], feat.at[y], feat_s, feat_r, partner)
    swap_feat.start()
    tail_out = [
        remote(tails.at[2], tails.at[y], tail_s.at[i], tail_r.at[i], tail_to[i]) for i in range(2)
    ]
    for copy in tail_out:
        copy.start()
    for s in STREAMS:
        share(s, 0).start()
    acc[...] = jnp.zeros_like(acc)
    ref = feat.at[yn - 1 - y]
    remote(ref, ref, feat_s, feat_r, partner).wait_recv()

    tile = min(512, chans)
    eager = (2 * rows) % 128 == 0

    def product(s, start, depth):
        owner, col = start // half, pl.multiple_of(start % half, depth)
        left = feat[owner, :, pl.ds(col, depth)]

        @pl.loop(0, chans // tile)
        def _(j):
            cut = pl.ds(pl.multiple_of(j * tile, tile), tile)
            acc[s, :, cut] += jnp.dot(
                left,
                w_all[s, pl.ds(pl.multiple_of(start, depth), depth), cut],
                preferred_element_type=jnp.float32,
            )

    def compute(t):
        for s in STREAMS[:4]:
            shared(s, t).wait_recv()
            if eager:
                product(s, first_row(chip_of(s, t)), 2 * rows)

    def pump(s, t):
        landed(s, t).wait_recv()

        @pl.when(t < n - 1)
        def _():
            hop(s, t + 1).start()

        share(s, t).start()

    @pl.loop(1, n)
    def _(t):
        for s in STREAMS[:4]:
            pump(s, t)
        for s in STREAMS[4:]:

            @pl.when(t == LAG)
            def _():
                hop(s, 1).start()

            @pl.when(t > LAG)
            def _():
                pump(s, t - LAG)

        compute(t - 1)

    compute(n - 1)
    if not eager:
        depth = min(256, half)

        @pl.loop(0, yn * half // depth)
        def _(i):
            for s in range(4):
                product(s, i * depth, depth)

    for i in range(2):
        ref = tails.at[y if i == 0 else yn - 1 - y]
        remote(ref, ref, tail_s.at[i], tail_r.at[i], tail_to[i]).wait_recv()
    cols = min(512, chans)
    blocks = chans // cols

    @pl.loop(0, blocks)
    def _(j):
        cut = pl.ds(pl.multiple_of(j * cols, cols), cols)
        edge = jnp.zeros((tails.shape[1], cols), jnp.float32)
        for owner in range(yn):
            edge += jnp.dot(
                tails[owner],
                w_all[1, owner * half : (owner + 1) * half, cut],
                preferred_element_type=jnp.float32,
            )
        halo[:, cut] = jnp.where(z > 0, edge, 0.0)

    steps = count // games
    seg = steps // SUB

    @pl.loop(0, games * blocks)
    def _(u):
        g, j = u // blocks, u % blocks
        for s in STREAMS[4:]:

            @pl.when(u == 0)
            def _():
                pump(s, n - 2)

            @pl.when(u == games * blocks - 1)
            def _():
                pump(s, n - 1)

        cut = pl.ds(pl.multiple_of(j * cols, cols), cols)
        scan_block(
            acc, halo[pl.ds(pl.multiple_of(g * SUB, SUB), SUB), cut], conv_w[:, cut], bias[:, cut], rates[:, cut],
            ends, carry_s, z, g, cut, cols, seg,
        )

    def relay(d, source):
        ref = ends.at[source]
        return remote(ref, ref, ends_s.at[d], ends_r.at[d], at(((z + d) % zn, x)))

    for d in range(1, zn):
        relay(d, z).start()
    for d in range(1, zn):
        relay(d, (z + zn - d) % zn).wait_recv()
    for g in range(games):
        run = jnp.zeros((1, chans), jnp.float32)
        for j in range(zn - 1):
            run = jnp.where(j < z, ends[j, g, 1:2, :] * run + ends[j, g, 0:1, :], run)
        state[g : g + 1, :] = run
    for g in range(games):
        run = state[g : g + 1, :]

        @pl.loop(0, steps // 16)
        def _(i):
            here = pl.ds(pl.multiple_of(g * steps + i * 16, 16), 16)
            mixed[here, :] = (acc[2, here, :] + acc[3, here, :] * run).astype(jnp.bfloat16)

    for s in STREAMS[4:]:

        @pl.loop(0, n)
        def _(t):
            shared(s, t).wait_recv()

    parts, own_rows, part = out_buf.shape
    mine = pl.ds(pl.multiple_of(y * own_rows, own_rows), own_rows)
    theirs = pl.ds(pl.multiple_of((yn - 1 - y) * own_rows, own_rows), own_rows)

    def down(which, j):
        return lax.dot_general(
            mixed[which, :],
            wd_all[j * part : (j + 1) * part, :],
            (((1,), (1,)), ((), ())),
            preferred_element_type=jnp.float32,
        )

    def exchange(j):
        return remote(out_buf.at[j], in_buf.at[j], out_s.at[j], out_r.at[j], partner)

    for j in range(parts):
        out_buf[j] = down(theirs, j).astype(jnp.bfloat16)
        if j:
            exchange(j - 1).start()
    kept[0] = down(mine, 0)
    exchange(parts - 1).start()
    for j in range(1, parts):
        kept[j] = down(mine, j)
    for j in range(parts):
        exchange(j).wait_recv()
        first = j * part
        base = feat[first // half, mine, first % half : first % half + part].astype(jnp.float32)
        total = kept[j] + in_buf[j].astype(jnp.float32)
        resid[:, first : first + part] = (base + total).astype(jnp.bfloat16)
    for j in range(parts):
        exchange(j).wait_send()
    for d in range(1, zn):
        relay(d, z).wait_send()

    for s in STREAMS:

        @pl.loop(1, n)
        def _(t):
            hop(s, t).wait_send()

        @pl.loop(0, n)
        def _(t):
            share(s, t).wait_send()

    swap_feat.wait_send()
    for copy in tail_out:
        copy.wait_send()


def scan_block(acc, halo, conv_w, bias, rates, ends, carry_s, z, g, cut, cols, seg):
    w = [conv_w[k : k + 1, :] for k in range(KERNEL)]
    b0, b1 = bias[0:1, :], bias[1:2, :]
    scale = -8.0 * rates
    row = lax.broadcasted_iota(jnp.int32, (SUB, cols), 0)

    def at(t):
        return pl.ds(pl.multiple_of((g * seg + t) * SUB, SUB), SUB)

    def before(j):
        rolled = pltpu.roll(acc[1, at(seg - j), cut], 1, 0)
        return jnp.where(row == 0, halo[KERNEL - 1 - j : KERNEL - j, :], rolled)

    def step(t, state):
        h, p, x1, x2, x3 = state
        here = at(t)
        x0 = acc[1, here, cut]
        conv = w[0] * x0 + w[1] * x1 + w[2] * x2 + w[3] * x3
        recur = jax.nn.sigmoid(acc[2, here, cut] + b0)
        inflow = jax.nn.sigmoid(acc[3, here, cut] + b1)
        a = jnp.exp(recur * scale)
        h = a * h + jnp.sqrt(1.0 - a * a) * inflow * conv
        p = a * p
        acc[0, here, cut] = jax.nn.gelu(acc[0, here, cut])
        acc[2, here, cut] = h
        acc[3, here, cut] = p
        return h, p, x0, x1, x2

    zero = jnp.zeros((SUB, cols), jnp.float32)
    h, p, _, _, _ = lax.fori_loop(
        0, seg, step, (zero, zero + 1.0, before(1), before(2), before(3)), unroll=4
    )
    run, dec = jnp.zeros((1, cols), jnp.float32), jnp.ones((1, cols), jnp.float32)
    for s in range(SUB):
        carry_s[0, s : s + 1, :] = run
        carry_s[1, s : s + 1, :] = dec
        run = p[s : s + 1] * run + h[s : s + 1]
        dec = p[s : s + 1] * dec
    ends[z, g, 0:1, cut] = run
    ends[z, g, 1:2, cut] = dec
    run, dec = carry_s[0], carry_s[1]

    def finish(t, _):
        here = at(t)
        gate, p = acc[0, here, cut], acc[3, here, cut]
        acc[2, here, cut] = (acc[2, here, cut] + p * run) * gate
        acc[3, here, cut] = p * dec * gate
        return 0

    lax.fori_loop(0, seg, finish, 0, unroll=4)


def core_block(emb, wb, wd, tail, conv_w, bias, rates, games):
    count, half = emb.shape
    rows, chans = wd.shape
    yn = lax.axis_size("width")
    n = lax.axis_size("tm") * (lax.axis_size("batch") // 2)
    depth = yn * half
    vmem = pl.BlockSpec(memory_space=pltpu.VMEM)
    hbm = pl.BlockSpec(memory_space=pl.ANY)
    dma = pltpu.SemaphoreType.DMA
    streams = len(STREAMS)
    zn = lax.axis_size("tm")
    own_rows = count // yn
    part = min(512, half)
    parts = depth // part
    return pl.pallas_call(
        core_kernel,
        in_specs=[hbm] * 4 + [vmem] * 3,
        out_specs=vmem,
        out_shape=jax.ShapeDtypeStruct((own_rows, depth), jnp.bfloat16),
        scratch_shapes=[
            pltpu.VMEM((4, depth, chans), jnp.bfloat16),
            pltpu.VMEM((4, count, chans), jnp.float32),
            pltpu.VMEM((3, games * SUB, half), jnp.bfloat16),
            pltpu.VMEM((games * SUB, chans), jnp.float32),
            pltpu.VMEM((2, SUB, min(512, chans)), jnp.float32),
            pltpu.VMEM((depth, chans), jnp.bfloat16),
            pltpu.VMEM((yn, count, half), jnp.bfloat16),
            pltpu.VMEM((zn, games, 2, chans), jnp.float32),
            pltpu.VMEM((games, chans), jnp.float32),
            pltpu.VMEM((count, chans), jnp.bfloat16),
            pltpu.VMEM((parts, own_rows, part), jnp.bfloat16),
            pltpu.VMEM((parts, own_rows, part), jnp.bfloat16),
            pltpu.VMEM((parts, own_rows, part), jnp.float32),
            dma((4,)), dma, dma, dma((2,)), dma((2,)),
            dma((streams, n)), dma((streams, n)), dma((streams, n)), dma((streams, n)),
            dma((zn,)), dma((zn,)), dma((parts,)), dma((parts,)),
        ],
        compiler_params=pltpu.CompilerParams(
            collective_id=0, has_side_effects=True, vmem_limit_bytes=56 * 1024 * 1024
        ),
        cost_estimate=pl.CostEstimate(
            flops=8 * count * chans * depth, bytes_accessed=200_000_000, transcendentals=8 * count * chans
        ),
    )(emb, wb, wd, tail, conv_w, bias, rates.reshape(1, chans))


def shards(
    moves,
    lengths,
    outcomes,
    embedded,
    w_branches,
    conv_w,
    gate_bias,
    rates,
    w_down,
    w_policy,
    w_value,
):
    games, block_len, half = embedded.shape
    count = games * block_len
    n_width = lax.axis_size("width")
    me = lax.axis_index("width")
    own_rows = count // n_width

    flat = interleave(embedded).reshape(count, half)
    heads = jnp.concatenate([w_policy, w_value[:, None]], 1)
    heads = both(heads, swap(heads, "width"), "width", 0)
    depth = n_width * half
    tail = flat.reshape(games, block_len // SUB, SUB, half)[:, 1 - KERNEL :, SUB - 1, :]
    tail = jnp.pad(tail, ((0, 0), (0, SUB + 1 - KERNEL), (0, 0))).reshape(games * SUB, half)
    resid = core_block(flat, w_branches, w_down, tail, conv_w, gate_bias, rates, games)
    here = lax.axis_index("tm")

    def mine(x):
        return lax.dynamic_slice_in_dim(x, me * own_rows, own_rows, 0)

    wide = resid.astype(jnp.float32)
    sumsq = jnp.sum(wide * wide, -1)
    scores = jnp.dot(resid, heads, preferred_element_type=jnp.float32)
    norm = lax.rsqrt(sumsq / depth + 1e-06)
    scores = scores * norm[:, None]
    logits = scores[:, :-1]
    value = jnp.tanh(scores[:, -1])
    top = jnp.max(logits, -1, keepdims=True)
    lse = top[:, 0] + jnp.log(jnp.sum(jnp.exp(logits - top), -1))
    column = lax.broadcasted_iota(jnp.int32, logits.shape, 1)
    picked = jnp.sum(jnp.where(column == mine(interleave(moves).reshape(count, 1)), logits, 0.0), -1)
    target = jnp.broadcast_to(outcomes.astype(jnp.float32)[:, None], (games, block_len))
    position = here * block_len + lax.broadcasted_iota(jnp.int32, (games, block_len), 1)
    live = interleave(position < lengths[:, None]).reshape(count)
    loss = jnp.where(mine(live), lse - picked + (value - mine(target.reshape(count))) ** 2, 0.0)
    result = jnp.stack([loss, value])
    result = both(result, swap(result, "width"), "width", 1)
    result = result.reshape(2, games, block_len)
    return (restore(result[0]), restore(result[1]))


def solution(mesh):
    in_specs = (
        P("batch", "tm"),
        P("batch"),
        P("batch"),
        P("batch", "tm", "width"),
        P(None, ("tm", "batch"), "width"),
        P(None, "width"),
        P(None, "width"),
        P("width"),
        P(("tm", "batch"), "width"),
        P("width", None),
        P("width"),
    )
    out_specs = (P("batch", "tm"), P("batch", "tm"))
    return jax.shard_map(shards, mesh=mesh, in_specs=in_specs, out_specs=out_specs, check_vma=False)
```

profile of v0, /device:TPU:0, one launch (start us, length us, event | category | flops | bytes accessed | tf_op | source)
XLA Modules:
  0.0 181.1 jit_solution(15521215281451857437)
XLA Ops:
  0.6 0.0 copy-start
  0.6 0.8 broadcast_in_dim.20
  1.4 1.2 pad_maximum_fusion
  2.6 3.1 %collective-permute-start = (bf16[1024,363]{0,1:T(8,128)(2,1)S(1)}, bf16[1024,363]{0,1:T(8,128)(2,1)S(1)}, u32[]{:S(2)}, u32[]{:S(2)}) collective-permute-start(bf16[1024,363]{0,1:T(8,128)(2,1)S(1)} %pad_maximum_fusion), channel_id=1, source_target_pairs={{0,1},{1,0},{2,3},{3,2},{4,5},{5,4},{6,7},{7,6},{8,9},{9,8},{10,11... | collective-permute-start | bytes 2230280 | tf_op jit(solution)/shard_map/ppermute | solution.py:17
  5.7 0.0 copy-done
  5.7 1.6 copy.19
  7.2 0.1 copy.26
  7.3 0.6 pad_bitcast_fusion.tail
  8.0 0.0 copy-start.4
  8.0 0.0 copy-start.5
  8.0 0.0 copy-start.3
  8.0 163.5 %shard_map.122 = bf16[256,2048]{1,0:T(8,128)(2,1)} custom-call(bf16[512,1024]{1,0:T(8,128)(2,1)} %bitcast.27, bf16[4,128,1024]{2,1,0:T(8,128)(2,1)} %wb.1, bf16[128,1024]{1,0:T(8,128)(2,1)} %wd.1, bf16[16,1024]{1,0:T(8,128)(2,1)} %pad_bitcast_fusion.tail, f32[4,1024]{1,0:T(4,128)} %conv_w.1, f32[2,1024]{1,0:T(2,128)} %bias.1, f32[1,1024]{1,0:T(1,128)} %bitcast.36), custom_call_target="tpu_custom_call" | custom-call | flops 8589934592 | bytes 200000000 | tf_op jit(solution)/shard_map/pallas_call | solution.py:375
  171.5 0.0 copy-done.4
  171.5 0.0 copy-start.1
  171.5 0.1 broadcast_compare_fusion
  171.6 0.1 lt.21
  171.7 0.0 copy-done.5
  171.7 0.1 broadcast_bitcast_fusion
  171.8 0.0 copy-done.3
  171.8 0.1 reshape.67
  171.9 0.1 copy.20
  172.0 0.1 reshape_reshape.8
  172.1 1.5 multiply_reduce_fusion
  173.6 0.0 copy-start.2
  173.6 0.0 collective-permute-done
  173.6 0.0 copy-done.1
  173.7 0.4 broadcast_select_fusion.1
  174.0 0.8 copy-done.2
  174.9 0.6 fusion.4
  175.5 0.1 slice_reduce_fusion
  175.5 0.1 exponential_reduce_fusion
  175.6 0.1 dynamic-slice_select_fusion
  175.7 0.6 collective-permute-start.1
  176.3 3.1 %collective-permute-done.1 = f32[2,256]{1,0:T(2,128)S(1)} collective-permute-done((f32[2,256]{1,0:T(2,128)S(1)}, f32[2,256]{1,0:T(2,128)S(1)}, u32[]{:S(2)}, u32[]{:S(2)}) %collective-permute-start.1) | collective-permute-done | bytes 2080 | tf_op jit(solution)/shard_map/ppermute | solution.py:17
  179.4 0.1 reshape_squeeze.6
  179.5 0.1 copy.21
  179.6 0.7 reshape.69
  180.3 0.1 reshape_squeeze.7
  180.3 0.1 copy.22
  180.4 0.7 reshape.70
  (10 shorter events, 0.1 us)
Async XLA Ops:
  0.6 5.0 %copy-start = (bf16[2,256,1024]{2,1,0:T(8,128)(2,1)S(1)}, bf16[2,256,1024]{2,1,0:T(8,128)(2,1)}, u32[]{:S(2)}) copy-start(bf16[2,256,1024]{2,1,0:T(8,128)(2,1)} %param.14) | copy-start | bytes 3145732
  2.6 171.0 %collective-permute-start = (bf16[1024,363]{0,1:T(8,128)(2,1)S(1)}, bf16[1024,363]{0,1:T(8,128)(2,1)S(1)}, u32[]{:S(2)}, u32[]{:S(2)}) collective-permute-start(bf16[1024,363]{0,1:T(8,128)(2,1)S(1)} %pad_maximum_fusion), channel_id=1, source_target_pairs={{0,1},{1,0},{2,3},{3,2},{4,5},{5,4},{6,7},{7,6},{8,9},{9,8},{10,11... | collective-permute-start | bytes 2230280 | tf_op jit(solution)/shard_map/ppermute | solution.py:17
  8.0 163.6 %copy-start.4 = (s32[2]{0:T(128)S(1)}, s32[2]{0:T(128)}, u32[]{:S(2)}) copy-start(s32[2]{0:T(128)} %param.12) | copy-start | bytes 28
  8.0 163.8 %copy-start.5 = (s32[2]{0:T(128)S(1)}, s32[2]{0:T(128)}, u32[]{:S(2)}) copy-start(s32[2]{0:T(128)} %param.13) | copy-start | bytes 28
  8.0 163.9 %copy-start.3 = (s32[2,256]{1,0:T(2,128)S(1)}, s32[2,256]{1,0:T(2,128)}, u32[]{:S(2)}) copy-start(s32[2,256]{1,0:T(2,128)} %param.11) | copy-start | bytes 6148
  171.5 2.1 %copy-start.1 = (bf16[1024,362]{0,1:T(8,128)(2,1)S(1)}, bf16[1024,362]{0,1:T(8,128)(2,1)}, u32[]{:S(2)}) copy-start(bf16[1024,362]{0,1:T(8,128)(2,1)} %param.20) | copy-start | bytes 2224132
  173.6 1.2 copy-start.2
  175.7 3.6 %collective-permute-start.1 = (f32[2,256]{1,0:T(2,128)S(1)}, f32[2,256]{1,0:T(2,128)S(1)}, u32[]{:S(2)}, u32[]{:S(2)}) collective-permute-start(f32[2,256]{1,0:T(2,128)S(1)} %pad_maximum_fusion.2), channel_id=1, source_target_pairs={{0,1},{1,0},{2,3},{3,2},{4,5},{5,4},{6,7},{7,6},{8,9},{9,8},{10,11... | collective-permute-start | bytes 6152 | tf_op jit(solution)/shard_map/ppermute | solution.py:17
where the time goes:
time: 181 us
  Pallas kernels  164 us (91%)
  local copies, waits for them, and re-layouts  5.97 us (3%)
  starting transfers between devices  3.61 us (2%)
  other arithmetic  3.47 us (2%)
  waiting for transfers between devices  3.1 us (2%)
    pallas_call x1, Pallas kernels, core_block(): pl.pallas_call(core_kernel, in_specs=[hbm] * 4 + [vmem] * 3, out_specs=vm...  164 us
  transfers between devices with their start and end apart: 2, of which 1 were waited for; matrix products, arithmetic and copies ran while one was open for 2% of the time, Pallas kernels for 90%

commit v1 on v0

v1 whole, which is shorter than its diff:
```python
import jax
import jax.numpy as jnp
from jax import lax
from jax.experimental import pallas as pl
from jax.experimental.pallas import tpu as pltpu
from jax.sharding import PartitionSpec as P

KERNEL = 4
SUB = 8
LANE = 128
MESH = pl.DeviceIdType.MESH
DIRS = (0, 1)
PAIRS = (0, 1)


def core_kernel(
    emb, wb, wd, heads_in, wval, conv_w, bias, rates, moves, lengths, outcomes,
    out_loss, out_value,
    w_all, wd_all, raw, feat, tail_buf, tails, acc, carry_s, ends, mix, mix_in, down, heads, wval_all, res,
    loc_w, loc_d, loc_e, loc_h, feat_s, feat_r, tail_s, tail_r, val_s, val_r, head_s, head_r, hrel_s, hrel_r,
    ring_s, ring_r, peer_s, peer_r, dring_s, dring_r, dpeer_s, dpeer_r, dpart_s, dpart_r, drel_s, drel_r,
    ends_s, ends_r, mix_s, mix_r, res_s, res_r,
):
    z, b, y = lax.axis_index("tm"), lax.axis_index("batch"), lax.axis_index("width")
    zn, bn, yn = lax.axis_size("tm"), lax.axis_size("batch"), lax.axis_size("width")
    x, core = b // 2, b % 2
    n = zn * (bn // 2)
    rows, chans = wd.shape
    games, steps, half = emb.shape
    depth = yn * half
    count = games * steps
    seg = steps // SUB
    chunks = chans // LANE
    wide = 2 * LANE
    items = chans // wide
    reach = n // 2
    per = n // 4
    other = yn - 1 - y

    def spot(r):
        cx = r // zn
        cz = r % zn
        return cz + (cx % 2) * (zn - 1 - 2 * cz), cx

    r = x * zn + z + (x % 2) * (zn - 1 - 2 * z)

    def at(place, c=core, w=y):
        return {"tm": place[0], "batch": place[1] * 2 + c, "width": w}

    ahead, behind = at(spot((r + 1) % n)), at(spot((r + n - 1) % n))
    peer = at((z, x), 1 - core)
    partner = at((z, x), core, other)
    after = ((z + 1) % zn, x)
    before = ((z + zn - 1) % zn, x)
    greet = [ahead, behind, peer, partner, at(after), at(after, core, other), at(before), at(before, core, other)]
    greet += [at(((z + d) % zn, x)) for d in range(2, zn - 1)]

    def first_row(chip):
        cz, cx = spot(chip)
        return (cz * bn + cx * 2) * rows

    def block(chip, c):
        return pl.ds(pl.multiple_of(first_row(chip) + c * rows, rows), rows)

    mine = block(r, core)

    def remote(src, dst, send, recv, device):
        return pltpu.make_async_remote_copy(
            src_ref=src, dst_ref=dst, send_sem=send, recv_sem=recv, device_id=device, device_id_type=MESH
        )

    def load_chunk(c):
        return [
            pltpu.make_async_copy(
                wb.at[m, :, pl.ds(pl.multiple_of(c * LANE, LANE), LANE)],
                w_all.at[c, m // 2, mine, (m % 2) * LANE : (m % 2 + 1) * LANE],
                loc_w.at[c],
            )
            for m in range(4)
        ]

    own_emb = pltpu.make_async_copy(emb, raw.at[y], loc_e)
    own_heads = pltpu.make_async_copy(heads_in, heads.at[pl.ds(pl.multiple_of(y * half, half), half), :], loc_h)
    for copy in load_chunk(0):
        copy.start()
    own_emb.start()
    for c in range(1, chunks):
        for copy in load_chunk(c):
            copy.start()
    for j in range(items):
        pltpu.make_async_copy(wd.at[:, j * wide : (j + 1) * wide], wd_all.at[j, y, mine, :], loc_d.at[j]).start()
    own_heads.start()
    ends[...] = jnp.zeros_like(ends)
    res[...] = jnp.zeros_like(res)
    wval_all[y] = wval[...]
    barrier = pltpu.get_barrier_semaphore()
    for device in greet:
        pl.semaphore_signal(barrier, inc=1, device_id=device, device_id_type=MESH)
    pl.semaphore_wait(barrier, len(greet))

    def chip_of(d, t):
        return (r + n - t) % n if d == 0 else (r + t) % n

    def toward(d):
        return ahead if d == 0 else behind

    def hops(which, d):
        return reach if which == d else n - 1 - reach

    def piece(c, p, chip):
        return w_all.at[c, p, block(chip, core), :]

    def hop(c, p, d, t):
        ref = piece(c, p, chip_of(d, t - 1))
        return remote(ref, ref, ring_s.at[c], ring_r.at[c, p, d, t - 1], toward(d))

    def landed(c, p, d, t):
        ref = piece(c, p, chip_of(d, t))
        return remote(ref, ref, ring_s.at[c], ring_r.at[c, p, d, t - 1], toward(d))

    def share(c, p, chip):
        ref = piece(c, p, chip)
        return remote(ref, ref, peer_s.at[c], peer_r.at[c], peer)

    def begin(c):
        ref = w_all.at[c, :, 0:rows, :]
        pltpu.make_async_copy(ref, ref, loc_w.at[c]).wait()
        for p in PAIRS:
            for d in DIRS:
                hop(c, p, d, 1).start()
        for p in PAIRS:
            share(c, p, r).start()

    def pump(c, t):
        for p, d in ((0, 0), (1, 1), (1, 0), (0, 1)):
            last = hops(p, d)

            @pl.when(t <= last)
            def _():
                landed(c, p, d, t).wait_recv()

                @pl.when(t < last)
                def _():
                    hop(c, p, d, t + 1).start()

                share(c, p, chip_of(d, t)).start()

    def dpiece(j, w, chip, c=core):
        return wd_all.at[j, w, block(chip, c), :]

    def dhop(j, d, t):
        ref = dpiece(j, y, chip_of(d, t - 1))
        return remote(ref, ref, dring_s.at[j], dring_r.at[j, d, t - 1], toward(d))

    def dlanded(j, d, t):
        ref = dpiece(j, y, chip_of(d, t))
        return remote(ref, ref, dring_s.at[j], dring_r.at[j, d, t - 1], toward(d))

    def dspread(j, chip):
        ref = dpiece(j, y, chip)
        remote(ref, ref, dpeer_s.at[j], dpeer_r.at[j], peer).start()
        remote(ref, ref, dpart_s.at[j], dpart_r.at[j, chip], partner).start()

    def dbegin(j):
        ref = wd_all.at[j, y, mine, :]
        pltpu.make_async_copy(ref, ref, loc_d.at[j]).wait()
        for d in DIRS:
            dhop(j, d, 1).start()
        dspread(j, r)

    def dpump(j, t):
        for d in DIRS:
            last = hops(j % 2, d)

            @pl.when((t >= 1) & (t <= last))
            def _():
                dlanded(j, d, t).wait_recv()

                @pl.when(t < last)
                def _():
                    dhop(j, d, t + 1).start()

                dspread(j, chip_of(d, t))

    def drelay(j, t):
        for d in DIRS:
            last = hops(j % 2, d)

            @pl.when((t >= d) & (t <= last))
            def _():
                ref = dpiece(j, other, chip_of(d, t))
                remote(ref, ref, dpart_s.at[j], dpart_r.at[j, chip_of(d, t)], partner).wait_recv()
                remote(ref, ref, drel_s.at[j], drel_r.at[j], peer).start()

    row_id = lax.broadcasted_iota(jnp.int32, (steps, steps), 0)
    lane_id = lax.broadcasted_iota(jnp.int32, (steps, steps), 1)
    spread = (row_id % SUB) * seg + row_id // SUB == lane_id

    def prepare():
        ref = raw.at[other]
        remote(ref, ref, feat_s, feat_r, partner).wait_recv()
        turn = jnp.where(spread, 1.0, 0.0).astype(jnp.bfloat16)
        for owner in range(yn):
            for g in range(games):
                feat[g * steps : (g + 1) * steps, owner * half : (owner + 1) * half] = jnp.dot(
                    turn, raw[owner, g], preferred_element_type=jnp.float32
                ).astype(jnp.bfloat16)

        @pl.when(z > 0)
        def _():
            for i in range(2):
                ref = tails.at[y if i == 0 else other]
                remote(ref, ref, tail_s.at[i], tail_r.at[i], peer).wait_recv()
            for owner in range(yn):
                feat[count : count + games * SUB, owner * half : (owner + 1) * half] = tails[owner]

        @pl.when(z == 0)
        def _():
            feat[count : count + games * SUB, :] = jnp.zeros((games * SUB, depth), jnp.bfloat16)

        down[...] = feat[pl.ds(pl.multiple_of(y * steps, steps), steps), :].astype(jnp.float32)

    def product(c):
        ref = w_all.at[c, :, 0 : n * rows, :]
        remote(ref, ref, peer_s.at[c], peer_r.at[c], peer).wait_recv()

        @pl.loop(0, 2)
        def _(p):
            acc[p] = jnp.dot(feat[...], w_all[c, p], preferred_element_type=jnp.float32)

    lo, hi = slice(0, LANE), slice(LANE, 2 * LANE)

    def lines(g, t):
        return pl.ds(pl.multiple_of(g * steps + t * SUB, SUB), SUB)

    def ends_copy(c, d, source, place):
        ref = ends.at[c, source]
        return remote(ref, ref, ends_s.at[c, d], ends_r.at[c, d], at(place))

    def scan(c):
        cut = pl.ds(pl.multiple_of(c * LANE, LANE), LANE)
        w = [conv_w[k : k + 1, cut] for k in range(KERNEL)]
        b0, b1 = bias[0:1, cut], bias[1:2, cut]
        scale = -8.0 * rates[:, cut]
        row = lax.broadcasted_iota(jnp.int32, (SUB, LANE), 0)

        def earlier(g, j):
            rolled = pltpu.roll(acc[0, lines(g, seg - j), hi], 1, 0)
            first = count + g * SUB + SUB - j
            return jnp.where(row == 0, acc[0, first : first + 1, hi], rolled)

        def step(t, state):
            new = []
            for g in range(games):
                h, p, x1, x2, x3 = state[g]
                here = lines(g, t)
                x0 = acc[0, here, hi]
                conv = w[0] * x0 + w[1] * x1 + w[2] * x2 + w[3] * x3
                recur = jax.nn.sigmoid(acc[1, here, lo] + b0)
                inflow = jax.nn.sigmoid(acc[1, here, hi] + b1)
                a = jnp.exp(recur * scale)
                h = a * h + jnp.sqrt(1.0 - a * a) * inflow * conv
                p = a * p
                acc[0, here, lo] = jax.nn.gelu(acc[0, here, lo])
                acc[1, here, lo] = h
                acc[1, here, hi] = p
                new.append((h, p, x0, x1, x2))
            return tuple(new)

        zero = jnp.zeros((SUB, LANE), jnp.float32)
        start = tuple((zero, zero + 1.0, earlier(g, 1), earlier(g, 2), earlier(g, 3)) for g in range(games))
        final = lax.fori_loop(0, seg, step, start, unroll=2)
        for g in range(games):
            h, p = final[g][:2]
            run, dec = jnp.zeros((1, LANE), jnp.float32), jnp.ones((1, LANE), jnp.float32)
            for s in range(SUB):
                carry_s[g, 0, s : s + 1, :] = run
                carry_s[g, 1, s : s + 1, :] = dec
                run = p[s : s + 1] * run + h[s : s + 1]
                dec = p[s : s + 1] * dec
            ends[c, z, 2 * g : 2 * g + 1, :] = run
            ends[c, z, 2 * g + 1 : 2 * g + 2, :] = dec
        for d in range(1, zn):

            @pl.when(z + d < zn)
            def _():
                ends_copy(c, d, z, (z + d, x)).start()

    def mix_copy(c):
        return remote(mix.at[c, other], mix_in.at[c], mix_s.at[c], mix_r.at[c], partner)

    def finish(c):
        for d in range(1, zn):

            @pl.when(z >= d)
            def _():
                ends_copy(c, d, z - d, (z - d, x)).wait_recv()

        for g in range(games):
            run = jnp.zeros((1, LANE), jnp.float32)
            for j in range(zn - 1):
                run = jnp.where(j < z, ends[c, j, 2 * g + 1 : 2 * g + 2, :] * run + ends[c, j, 2 * g : 2 * g + 1, :], run)
            enter = carry_s[g, 0] + carry_s[g, 1] * run
            enter = jnp.concatenate([enter, enter], 0)
            for i in range(steps // 16):
                here = slice(g * steps + i * 16, g * steps + (i + 1) * 16)
                value = (acc[1, here, lo] + acc[1, here, hi] * enter) * acc[0, here, lo]
                mix[c, g, i * 16 : (i + 1) * 16, :] = value.astype(jnp.bfloat16)
        mix_copy(c).start()

    def project(j):
        for c in (2 * j, 2 * j + 1):
            mix_copy(c).wait_recv()
        ref = wd_all.at[j, y, 0 : n * rows, :]
        remote(ref, ref, dpeer_s.at[j], dpeer_r.at[j], peer).wait_recv()
        remote(ref, ref, drel_s.at[j], drel_r.at[j], peer).wait_recv()
        own = jnp.concatenate([mix[2 * j, y], mix[2 * j + 1, y]], 1)
        theirs = jnp.concatenate([mix_in[2 * j], mix_in[2 * j + 1]], 1)
        part = min(512, half)

        @pl.loop(0, depth // part)
        def _(f):
            cut = pl.ds(pl.multiple_of(f * part, part), part)
            total = down[:, cut]
            for left, w in ((own, y), (theirs, other)):
                total += lax.dot_general(
                    left, wd_all[j, w, cut, :], (((1,), (1,)), ((), ())), preferred_element_type=jnp.float32
                )
            down[:, cut] = total

    begin(0)
    swap_feat = remote(emb, raw.at[y], feat_s, feat_r, partner)
    swap_feat.start()
    swap_val = remote(wval, wval_all.at[y], val_s, val_r, partner)
    swap_val.start()
    own_emb.wait()
    last = [raw[y, g, steps - 16 : steps, :].astype(jnp.float32)[16 - SUB :] for g in range(games)]
    tail_buf[...] = jnp.concatenate(last, 0).astype(jnp.bfloat16)

    def tail_copy(i):
        return remote(tail_buf, tails.at[y], tail_s.at[i], tail_r.at[i], at(after, core, y if i == 0 else other))

    @pl.when(z < zn - 1)
    def _():
        for i in range(2):
            tail_copy(i).start()

    own_heads.wait()
    quarter = half // 2

    def head_rows(w, c):
        return heads.at[pl.ds(pl.multiple_of(w * half + c * quarter, quarter), quarter), :]

    def relay_heads_wait():
        remote(head_rows(other, core), head_rows(other, core), head_s, head_r, partner).wait_recv()

    swap_heads = remote(head_rows(y, core), head_rows(y, core), head_s, head_r, partner)
    relay_heads = remote(head_rows(other, core), head_rows(other, core), hrel_s, hrel_r, peer)
    first_d = [per + j * ((chunks - 2) * per - reach) // max(items - 1, 1) for j in range(items)]

    @pl.loop(0, chunks + 4)
    def _(k):
        @pl.loop(0, per)
        def _(i):
            slot = k * per + i
            for j in range(items):

                @pl.when(slot == first_d[j])
                def _():
                    dbegin(j)

            @pl.when((i == per - 1) & (k < chunks - 1))
            def _():
                begin(k + 1)

            @pl.when((k >= 1) & (k <= chunks))
            def _():
                pump(k - 1, per + i + 1)

            @pl.when(k < chunks)
            def _():
                pump(k, i + 1)

            for j in range(items):
                t = slot - first_d[j]
                dpump(j, t)
                drelay(j, t - 1)

            @pl.when(i == 0)
            def _():
                @pl.when((k >= 3) & (k < chunks + 3))
                def _():
                    finish(k - 3)

            @pl.when((k == 2) & (i == per - 1))
            def _():
                prepare()
                swap_heads.start()

            @pl.when((k == 5) & (i == per - 1))
            def _():
                relay_heads_wait()
                relay_heads.start()

            @pl.when(((i == 0) & (k >= 3) & (k < chunks + 2)) | ((i == per - 1) & (k == 2)))
            def _():
                product(k - 2)

            @pl.when(i == per - 1)
            def _():
                @pl.when((k >= 2) & (k < chunks + 2))
                def _():
                    scan(k - 2)

                @pl.when((k >= 5) & (k % 2 == 1))
                def _():
                    project((k - 5) // 2)

    remote(head_rows(other, 1 - core), head_rows(other, 1 - core), hrel_s, hrel_r, peer).wait_recv()
    ref = wval_all.at[other]
    remote(ref, ref, val_s, val_r, partner).wait_recv()
    resid = down[...].astype(jnp.bfloat16)
    full = resid.astype(jnp.float32)
    sumsq = jnp.sum(full * full, -1, keepdims=True)
    row = jnp.concatenate([wval_all[owner, 0:1, :] for owner in range(yn)], 1)
    score = jnp.sum(full * row, -1, keepdims=True)
    norm = lax.rsqrt(sumsq / depth + 1e-06)
    logits = jnp.dot(resid, heads[...], preferred_element_type=jnp.float32) * norm
    value = jnp.tanh(score * norm)
    top = jnp.max(logits, -1, keepdims=True)
    lse = top + jnp.log(jnp.sum(jnp.exp(logits - top), -1, keepdims=True))
    played = moves[pl.ds(y, 1), :].astype(jnp.float32)
    played = jnp.sum(jnp.where(spread, played, 0.0), -1, keepdims=True)
    column = lax.broadcasted_iota(jnp.int32, logits.shape, 1).astype(jnp.float32)
    picked = jnp.sum(jnp.where(column == played, logits, 0.0), -1, keepdims=True)
    target = outcomes[y].astype(jnp.float32)
    loss = lse - picked + (value - target) ** 2
    loss = jnp.sum(jnp.where(spread, loss, 0.0), 0, keepdims=True)
    value = jnp.sum(jnp.where(spread, value, 0.0), 0, keepdims=True)
    position = z * steps + lax.broadcasted_iota(jnp.int32, (1, steps), 1)
    loss = jnp.where(position < lengths[y], loss, 0.0)
    res[y, 0:1, :] = loss
    res[y, 1:2, :] = value
    swap_res = remote(res.at[y], res.at[y], res_s, res_r, partner)
    swap_res.start()
    ref = res.at[other]
    remote(ref, ref, res_s, res_r, partner).wait_recv()
    for owner in range(yn):
        out_loss[owner : owner + 1, :] = res[owner, 0:1, :]
        out_value[owner : owner + 1, :] = res[owner, 1:2, :]

    swap_res.wait_send()
    swap_feat.wait_send()
    swap_val.wait_send()
    swap_heads.wait_send()
    relay_heads.wait_send()

    @pl.when(z < zn - 1)
    def _():
        for i in range(2):
            tail_copy(i).wait_send()

    @pl.loop(0, chunks)
    def _(c):
        ref = w_all.at[c, :, 0 : (n - 1) * rows, :]
        remote(ref, ref, ring_s.at[c], peer_r.at[c], peer).wait_send()
        ref = w_all.at[c, :, 0 : n * rows, :]
        remote(ref, ref, peer_s.at[c], peer_r.at[c], peer).wait_send()
        mix_copy(c).wait_send()
        for d in range(1, zn):

            @pl.when(z + d < zn)
            def _():
                ends_copy(c, d, z, (z + d, x)).wait_send()

    @pl.loop(0, items)
    def _(j):
        ref = wd_all.at[j, y, 0 : (n - 1) * rows, :]
        remote(ref, ref, dring_s.at[j], dpeer_r.at[j], peer).wait_send()
        ref = wd_all.at[j, y, 0 : n * rows, :]
        for sem in (dpeer_s, dpart_s, drel_s):
            remote(ref, ref, sem.at[j], dpeer_r.at[j], peer).wait_send()


def core_block(emb, wb, wd, heads, wval, conv_w, bias, rates, moves, lengths, outcomes):
    games, steps, half = emb.shape
    rows, chans = wd.shape
    yn, zn = lax.axis_size("width"), lax.axis_size("tm")
    n = zn * (lax.axis_size("batch") // 2)
    depth, count = yn * half, games * steps
    labels = heads.shape[1]
    assert games == yn and n % 4 == 0
    chunks, wide = chans // LANE, 2 * LANE
    items, reach = chans // wide, n // 2
    vmem = pl.BlockSpec(memory_space=pltpu.VMEM)
    smem = pl.BlockSpec(memory_space=pltpu.SMEM)
    hbm = pl.BlockSpec(memory_space=pl.ANY)
    dma = pltpu.SemaphoreType.DMA
    f32, b16 = jnp.float32, jnp.bfloat16
    return pl.pallas_call(
        core_kernel,
        in_specs=[hbm] * 4 + [vmem] * 5 + [smem] * 2,
        out_specs=(vmem, vmem),
        out_shape=(jax.ShapeDtypeStruct((games, steps), f32), jax.ShapeDtypeStruct((games, steps), f32)),
        scratch_shapes=[
            pltpu.VMEM((chunks, 2, depth, wide), b16),
            pltpu.VMEM((items, yn, depth, wide), b16),
            pltpu.VMEM((yn, games, steps, half), b16),
            pltpu.VMEM((count + games * SUB, depth), b16),
            pltpu.VMEM((games * SUB, half), b16),
            pltpu.VMEM((yn, games * SUB, half), b16),
            pltpu.VMEM((2, count + games * SUB, wide), f32),
            pltpu.VMEM((games, 2, SUB, LANE), f32),
            pltpu.VMEM((chunks, zn, SUB, LANE), f32),
            pltpu.VMEM((chunks, games, steps, LANE), b16),
            pltpu.VMEM((chunks, steps, LANE), b16),
            pltpu.VMEM((steps, depth), f32),
            pltpu.VMEM((depth, labels), b16),
            pltpu.VMEM((yn, SUB, half), f32),
            pltpu.VMEM((yn, SUB, steps), f32),
            dma((chunks,)), dma((items,)), dma, dma, dma, dma, dma((2,)), dma((2,)), dma, dma, dma, dma, dma, dma,
            dma((chunks,)), dma((chunks, 2, 2, reach)), dma((chunks,)), dma((chunks,)),
            dma((items,)), dma((items, 2, reach)), dma((items,)), dma((items,)),
            dma((items,)), dma((items, n)), dma((items,)), dma((items,)),
            dma((chunks, zn)), dma((chunks, zn)), dma((chunks,)), dma((chunks,)), dma, dma,
        ],
        compiler_params=pltpu.CompilerParams(
            collective_id=0, has_side_effects=True, vmem_limit_bytes=56 * 1024 * 1024
        ),
        cost_estimate=pl.CostEstimate(
            flops=8 * count * chans * depth, bytes_accessed=200_000_000, transcendentals=8 * count * chans
        ),
    )(emb, wb, wd, heads, wval, conv_w, bias, rates, moves, lengths, outcomes)


def shards(
    moves,
    lengths,
    outcomes,
    embedded,
    w_branches,
    conv_w,
    gate_bias,
    rates,
    w_down,
    w_policy,
    w_value,
):
    wval = jnp.broadcast_to(w_value.astype(jnp.float32)[None, :], (SUB, w_value.shape[0]))
    return core_block(
        embedded, w_branches, w_down, w_policy, wval, conv_w, gate_bias, rates.reshape(1, -1), moves, lengths, outcomes
    )


def solution(mesh):
    in_specs = (
        P("batch", "tm"),
        P("batch"),
        P("batch"),
        P("batch", "tm", "width"),
        P(None, ("tm", "batch"), "width"),
        P(None, "width"),
        P(None, "width"),
        P("width"),
        P(("tm", "batch"), "width"),
        P("width", None),
        P("width"),
    )
    out_specs = (P("batch", "tm"), P("batch", "tm"))
    return jax.shard_map(shards, mesh=mesh, in_specs=in_specs, out_specs=out_specs, check_vma=False)
```

time: 181 us -> 144 us (0.80)
  Pallas kernels: 164 us -> 138 us
  starting transfers between devices: 3.61 us -> 0 us
  other arithmetic: 3.47 us -> 0 us
  waiting for transfers between devices: 3.1 us -> 0 us
    pallas_call x1, Pallas kernels: 164 us -> 138 us  [core_block(): pl.pallas_call(core_kernel, in_specs=[hbm] * 4 + [vmem] * 5 + [smem] * 2,...]
    ppermute x2 -> x0, starting transfers between devices: 3.61 us -> none  [swap(): return lax.ppermute(value, axis, [(i, n - 1 - i) for i in range(n)])]
    unnamed x14 -> x7, local copies, waits for them, and re-layouts: 0.92 us -> 4.21 us
    ppermute x2 -> x0, waiting for transfers between devices: 3.1 us -> none  [swap(): return lax.ppermute(value, axis, [(i, n - 1 - i) for i in range(n)])]
    reshape x6 -> x0, local copies, waits for them, and re-layouts: 2.18 us -> none  [the longest x2 1.33 us: restore(): jnp.swapaxes(x.reshape(games, steps // SUB, SUB, *x.shape[2:]), 1, 2)]
  transfers between devices with their start and end apart: 2 -> 0, of which waited for: 1 -> 0; matrix products, arithmetic and copies ran while one was open for 2% -> 0% of each run, Pallas kernels for 90% -> 0%
where the time goes in v1:
time: 144 us
  Pallas kernels  138 us (96%)
  local copies, waits for them, and re-layouts  5.5 us (4%)
    pallas_call x1, Pallas kernels, core_block(): pl.pallas_call(core_kernel, in_specs=[hbm] * 4 + [vmem] * 5 + [smem] * 2,...  138 us
    unnamed x7, local copies, waits for them, and re-layouts  4.21 us

profile of v1, /device:TPU:0, one launch (start us, length us, event | category | flops | bytes accessed | tf_op | source)
XLA Modules:
  0.0 144.2 jit_solution(4949437848777665636)
XLA Ops:
  0.6 1.3 broadcast_in_dim.2.wval
  1.9 2.3 %copy.13.heads_in = bf16[1024,362]{1,0:T(8,128)(2,1)} copy(bf16[1024,362]{0,1:T(8,128)(2,1)} %param.20) | data formatting | bytes 1482752 | tf_op args[9]
  4.2 138.0 %shard_map.122 = (f32[2,256]{1,0:T(2,128)}, f32[2,256]{1,0:T(2,128)}) custom-call(bf16[2,256,1024]{2,1,0:T(8,128)(2,1)} %emb.1, bf16[4,128,1024]{2,1,0:T(8,128)(2,1)} %wb.1, bf16[128,1024]{1,0:T(8,128)(2,1)} %wd.1, bf16[1024,362]{1,0:T(8,128)(2,1)} %copy.13.heads_in, f32[8,1024]{1,0:T(8,128)} %broadcast_in_dim.2.wval, f32[4,1024]{1,0:T(4,128)} %conv_w.1, ...), custom_call_target="tpu_custom_call" | custom-call | flops 8589934592 | bytes 200000000 | tf_op jit(solution)/shard_map/pallas_call | solution.py:500
  142.3 0.0 copy-start.1
  142.3 0.7 copy-done.1
  142.9 0.0 copy-start
  142.9 0.6 copy.16
  143.5 0.1 copy-done
  143.6 0.6 copy.17
Async XLA Ops:
  142.3 0.7 copy-start.1
  142.9 0.7 copy-start

commit v2 on v1

--- a/solution.py
+++ b/solution.py
@@ -15,7 +15,7 @@
 
 def core_kernel(
     emb, wb, wd, heads_in, wval, conv_w, bias, rates, moves, lengths, outcomes,
-    out_loss, out_value,
+    out,
     w_all, wd_all, raw, feat, tail_buf, tails, acc, carry_s, ends, mix, mix_in, down, heads, wval_all, res,
     loc_w, loc_d, loc_e, loc_h, feat_s, feat_r, tail_s, tail_r, val_s, val_r, head_s, head_r, hrel_s, hrel_r,
     ring_s, ring_r, peer_s, peer_r, dring_s, dring_r, dpeer_s, dpeer_r, dpart_s, dpart_r, drel_s, drel_r,
@@ -80,7 +80,7 @@
         ]
 
     own_emb = pltpu.make_async_copy(emb, raw.at[y], loc_e)
-    own_heads = pltpu.make_async_copy(heads_in, heads.at[pl.ds(pl.multiple_of(y * half, half), half), :], loc_h)
+    own_heads = pltpu.make_async_copy(heads_in, heads.at[y], loc_h)
     for copy in load_chunk(0):
         copy.start()
     own_emb.start()
@@ -243,35 +243,52 @@
         b0, b1 = bias[0:1, cut], bias[1:2, cut]
         scale = -8.0 * rates[:, cut]
         row = lax.broadcasted_iota(jnp.int32, (SUB, LANE), 0)
+        tall = min(64, steps)
 
         def earlier(g, j):
             rolled = pltpu.roll(acc[0, lines(g, seg - j), hi], 1, 0)
             first = count + g * SUB + SUB - j
             return jnp.where(row == 0, acc[0, first : first + 1, hi], rolled)
 
+        for g in range(games):
+            old = [earlier(g, j) for j in range(KERNEL)[:0:-1]]
+            for i in range(steps // tall):
+                first = g * steps + i * tall
+                here = slice(first, first + tall)
+                x0 = acc[0, here, hi]
+                conv = w[0] * x0
+                for j in range(1, KERNEL):
+                    if i:
+                        xj = acc[0, first - j * SUB : first - j * SUB + tall, hi]
+                    else:
+                        xj = jnp.concatenate(old[KERNEL - 1 - j :] + [x0[: tall - j * SUB]], 0)
+                    conv += w[j] * xj
+                recur = 0.5 * jnp.tanh(0.5 * (acc[1, here, lo] + b0)) + 0.5
+                inflow = 0.5 * jnp.tanh(0.5 * (acc[1, here, hi] + b1)) + 0.5
+                a = jnp.exp(recur * scale)
+                left = 1.0 - a * a
+                root = left * lax.rsqrt(jnp.maximum(left, 1e-30))
+                acc[0, here, lo] = jax.nn.gelu(acc[0, here, lo])
+                acc[1, here, lo] = a
+                acc[1, here, hi] = root * inflow * conv
+
         def step(t, state):
             new = []
             for g in range(games):
-                h, p, x1, x2, x3 = state[g]
+                h, p = state[g]
                 here = lines(g, t)
-                x0 = acc[0, here, hi]
-                conv = w[0] * x0 + w[1] * x1 + w[2] * x2 + w[3] * x3
-                recur = jax.nn.sigmoid(acc[1, here, lo] + b0)
-                inflow = jax.nn.sigmoid(acc[1, here, hi] + b1)
-                a = jnp.exp(recur * scale)
-                h = a * h + jnp.sqrt(1.0 - a * a) * inflow * conv
+                a = acc[1, here, lo]
+                h = a * h + acc[1, here, hi]
                 p = a * p
-                acc[0, here, lo] = jax.nn.gelu(acc[0, here, lo])
-                acc[1, here, lo] = h
-                acc[1, here, hi] = p
-                new.append((h, p, x0, x1, x2))
+                acc[1, here, lo] = p
+                acc[1, here, hi] = h
+                new.append((h, p))
             return tuple(new)
 
         zero = jnp.zeros((SUB, LANE), jnp.float32)
-        start = tuple((zero, zero + 1.0, earlier(g, 1), earlier(g, 2), earlier(g, 3)) for g in range(games))
-        final = lax.fori_loop(0, seg, step, start, unroll=2)
+        final = lax.fori_loop(0, seg, step, tuple((zero, zero + 1.0) for g in range(games)), unroll=8)
         for g in range(games):
-            h, p = final[g][:2]
+            h, p = final[g]
             run, dec = jnp.zeros((1, LANE), jnp.float32), jnp.ones((1, LANE), jnp.float32)
             for s in range(SUB):
                 carry_s[g, 0, s : s + 1, :] = run
@@ -304,7 +321,7 @@
             enter = jnp.concatenate([enter, enter], 0)
             for i in range(steps // 16):
                 here = slice(g * steps + i * 16, g * steps + (i + 1) * 16)
-                value = (acc[1, here, lo] + acc[1, here, hi] * enter) * acc[0, here, lo]
+                value = (acc[1, here, hi] + acc[1, here, lo] * enter) * acc[0, here, lo]
                 mix[c, g, i * 16 : (i + 1) * 16, :] = value.astype(jnp.bfloat16)
         mix_copy(c).start()
 
@@ -329,6 +346,7 @@
             down[:, cut] = total
 
     begin(0)
+    begin(1)
     swap_feat = remote(emb, raw.at[y], feat_s, feat_r, partner)
     swap_feat.start()
     swap_val = remote(wval, wval_all.at[y], val_s, val_r, partner)
@@ -349,7 +367,7 @@
     quarter = half // 2
 
     def head_rows(w, c):
-        return heads.at[pl.ds(pl.multiple_of(w * half + c * quarter, quarter), quarter), :]
+        return heads.at[w, :, pl.ds(pl.multiple_of(c * quarter, quarter), quarter)]
 
     def relay_heads_wait():
         remote(head_rows(other, core), head_rows(other, core), head_s, head_r, partner).wait_recv()
@@ -369,29 +387,23 @@
                 def _():
                     dbegin(j)
 
-            @pl.when((i == per - 1) & (k < chunks - 1))
-            def _():
-                begin(k + 1)
+            @pl.when((i == per - 1) & (k < chunks - 2))
+            def _():
+                begin(k + 2)
+
+            @pl.when(k < chunks)
+            def _():
+                pump(k, i + 1)
 
             @pl.when((k >= 1) & (k <= chunks))
             def _():
                 pump(k - 1, per + i + 1)
-
-            @pl.when(k < chunks)
-            def _():
-                pump(k, i + 1)
 
             for j in range(items):
                 t = slot - first_d[j]
                 dpump(j, t)
                 drelay(j, t - 1)
 
-            @pl.when(i == 0)
-            def _():
-                @pl.when((k >= 3) & (k < chunks + 3))
-                def _():
-                    finish(k - 3)
-
             @pl.when((k == 2) & (i == per - 1))
             def _():
                 prepare()
@@ -402,19 +414,18 @@
                 relay_heads_wait()
                 relay_heads.start()
 
+            @pl.when((i == per - 1) & (k >= 5) & (k % 2 == 1))
+            def _():
+                project((k - 5) // 2)
+
+            @pl.when(((i == 0) & (k == 3)) | ((i == per - 1) & (k >= 3) & (k < chunks + 2)))
+            def _():
+                finish(k - 2 - jnp.where(i == 0, 1, 0))
+
             @pl.when(((i == 0) & (k >= 3) & (k < chunks + 2)) | ((i == per - 1) & (k == 2)))
             def _():
                 product(k - 2)
-
-            @pl.when(i == per - 1)
-            def _():
-                @pl.when((k >= 2) & (k < chunks + 2))
-                def _():
-                    scan(k - 2)
-
-                @pl.when((k >= 5) & (k % 2 == 1))
-                def _():
-                    project((k - 5) // 2)
+                scan(k - 2)
 
     remote(head_rows(other, 1 - core), head_rows(other, 1 - core), hrel_s, hrel_r, peer).wait_recv()
     ref = wval_all.at[other]
@@ -422,10 +433,18 @@
     resid = down[...].astype(jnp.bfloat16)
     full = resid.astype(jnp.float32)
     sumsq = jnp.sum(full * full, -1, keepdims=True)
-    row = jnp.concatenate([wval_all[owner, 0:1, :] for owner in range(yn)], 1)
+    row = [wval_all[owner].astype(jnp.float32) for owner in range(yn)]
+    row = jnp.concatenate([part[i : i + 1, :] for part in row for i in range(half // LANE)], 1)
     score = jnp.sum(full * row, -1, keepdims=True)
     norm = lax.rsqrt(sumsq / depth + 1e-06)
-    logits = jnp.dot(resid, heads[...], preferred_element_type=jnp.float32) * norm
+    logits = sum(
+        lax.dot_general(
+            resid[:, owner * half : (owner + 1) * half], heads[owner], (((1,), (1,)), ((), ())),
+            preferred_element_type=jnp.float32,
+        )
+        for owner in range(yn)
+    )
+    logits = logits * norm
     value = jnp.tanh(score * norm)
     top = jnp.max(logits, -1, keepdims=True)
     lse = top + jnp.log(jnp.sum(jnp.exp(logits - top), -1, keepdims=True))
@@ -446,8 +465,8 @@
     ref = res.at[other]
     remote(ref, ref, res_s, res_r, partner).wait_recv()
     for owner in range(yn):
-        out_loss[owner : owner + 1, :] = res[owner, 0:1, :]
-        out_value[owner : owner + 1, :] = res[owner, 1:2, :]
+        out[owner : owner + 1, :] = res[owner, 0:1, :]
+        out[games + owner : games + owner + 1, :] = res[owner, 1:2, :]
 
     swap_res.wait_send()
     swap_feat.wait_send()
@@ -488,7 +507,7 @@
     yn, zn = lax.axis_size("width"), lax.axis_size("tm")
     n = zn * (lax.axis_size("batch") // 2)
     depth, count = yn * half, games * steps
-    labels = heads.shape[1]
+    labels = heads.shape[0]
     assert games == yn and n % 4 == 0
     chunks, wide = chans // LANE, 2 * LANE
     items, reach = chans // wide, n // 2
@@ -500,8 +519,8 @@
     return pl.pallas_call(
         core_kernel,
         in_specs=[hbm] * 4 + [vmem] * 5 + [smem] * 2,
-        out_specs=(vmem, vmem),
-        out_shape=(jax.ShapeDtypeStruct((games, steps), f32), jax.ShapeDtypeStruct((games, steps), f32)),
+        out_specs=vmem,
+        out_shape=jax.ShapeDtypeStruct((2 * games, steps), f32),
         scratch_shapes=[
             pltpu.VMEM((chunks, 2, depth, wide), b16),
             pltpu.VMEM((items, yn, depth, wide), b16),
@@ -515,8 +534,8 @@
             pltpu.VMEM((chunks, games, steps, LANE), b16),
             pltpu.VMEM((chunks, steps, LANE), b16),
             pltpu.VMEM((steps, depth), f32),
-            pltpu.VMEM((depth, labels), b16),
-            pltpu.VMEM((yn, SUB, half), f32),
+            pltpu.VMEM((yn, labels, half), b16),
+            pltpu.VMEM((yn, half // LANE, LANE), b16),
             pltpu.VMEM((yn, SUB, steps), f32),
             dma((chunks,)), dma((items,)), dma, dma, dma, dma, dma((2,)), dma((2,)), dma, dma, dma, dma, dma, dma,
             dma((chunks,)), dma((chunks, 2, 2, reach)), dma((chunks,)), dma((chunks,)),
@@ -546,10 +565,12 @@
     w_policy,
     w_value,
 ):
-    wval = jnp.broadcast_to(w_value.astype(jnp.float32)[None, :], (SUB, w_value.shape[0]))
-    return core_block(
-        embedded, w_branches, w_down, w_policy, wval, conv_w, gate_bias, rates.reshape(1, -1), moves, lengths, outcomes
+    wval = w_value.reshape(-1, LANE)
+    out = core_block(
+        embedded, w_branches, w_down, w_policy.T, wval, conv_w, gate_bias, rates.reshape(1, -1), moves, lengths, outcomes
     )
+    games = embedded.shape[0]
+    return out[:games], out[games:]
 
 
 def solution(mesh):

time: 144 us -> 135 us (0.938)
  Pallas kernels: 138 us -> 132 us
  local copies, waits for them, and re-layouts: 5.5 us -> 1.33 us
    pallas_call x1, Pallas kernels: 138 us -> 132 us  [core_block(): pl.pallas_call(core_kernel, in_specs=[hbm] * 4 + [vmem] * 5 + [smem] * 2,...]
    unnamed x7 -> x0, local copies, waits for them, and re-layouts: 4.21 us -> none
where the time goes in v2:
time: 135 us; the launch traced here: 134 us
  Pallas kernels  132 us (98%)
    pallas_call x1, Pallas kernels, core_block(): pl.pallas_call(core_kernel, in_specs=[hbm] * 4 + [vmem] * 5 + [smem] * 2,...  132 us

profile of v2, /device:TPU:0, one launch (start us, length us, event | category | flops | bytes accessed | tf_op | source)
XLA Modules:
  0.0 134.4 jit_solution(16304295593830548645)
XLA Ops:
  0.6 132.5 %shard_map.122 = f32[4,256]{1,0:T(4,128)} custom-call(bf16[2,256,1024]{2,1,0:T(8,128)(2,1)} %emb.1, bf16[4,128,1024]{2,1,0:T(8,128)(2,1)} %wb.1, bf16[128,1024]{1,0:T(8,128)(2,1)} %wd.1, bf16[362,1024]{1,0:T(8,128)(2,1)} %bitcast.3, bf16[8,128]{1,0:T(8,128)(2,1)} %bitcast.5, f32[4,1024]{1,0:T(4,128)} %conv_w.1, f32[2,1024]{1,0:T(2,128)} %bias.1, ...), custom_call_target="tpu_custom_call" | custom-call | flops 8589934592 | bytes 200000000 | tf_op jit(solution)/shard_map/pallas_call | solution.py:519
  133.1 1.3 fusion

commit v3 on v2

--- a/solution.py
+++ b/solution.py
@@ -64,6 +64,10 @@
 
     mine = block(r, core)
 
+    def dpiece(j, w, chip):
+        cz, cx = spot(chip)
+        return wd_all.at[j, w, cz * (bn // 2) + cx, core]
+
     def remote(src, dst, send, recv, device):
         return pltpu.make_async_remote_copy(
             src_ref=src, dst_ref=dst, send_sem=send, recv_sem=recv, device_id=device, device_id_type=MESH
@@ -74,10 +78,17 @@
             pltpu.make_async_copy(
                 wb.at[m, :, pl.ds(pl.multiple_of(c * LANE, LANE), LANE)],
                 w_all.at[c, m // 2, mine, (m % 2) * LANE : (m % 2 + 1) * LANE],
-                loc_w.at[c],
+                loc_w,
             )
             for m in range(4)
         ]
+
+    ends[...] = jnp.zeros_like(ends)
+    res[...] = jnp.zeros_like(res)
+    wval_all[y] = wval[...]
+    barrier = pltpu.get_barrier_semaphore()
+    for device in greet:
+        pl.semaphore_signal(barrier, inc=1, device_id=device, device_id_type=MESH)
 
     own_emb = pltpu.make_async_copy(emb, raw.at[y], loc_e)
     own_heads = pltpu.make_async_copy(heads_in, heads.at[y], loc_h)
@@ -88,15 +99,13 @@
         for copy in load_chunk(c):
             copy.start()
     for j in range(items):
-        pltpu.make_async_copy(wd.at[:, j * wide : (j + 1) * wide], wd_all.at[j, y, mine, :], loc_d.at[j]).start()
+        pltpu.make_async_copy(wd.at[:, j * wide : (j + 1) * wide], dpiece(j, y, r), loc_d).start()
     own_heads.start()
-    ends[...] = jnp.zeros_like(ends)
-    res[...] = jnp.zeros_like(res)
-    wval_all[y] = wval[...]
-    barrier = pltpu.get_barrier_semaphore()
-    for device in greet:
-        pl.semaphore_signal(barrier, inc=1, device_id=device, device_id_type=MESH)
     pl.semaphore_wait(barrier, len(greet))
+    ref = w_all.at[:, :, 0:rows, :]
+    pltpu.make_async_copy(ref, ref, loc_w).wait()
+    ref = wd_all.at[:, 0, 0, 0]
+    pltpu.make_async_copy(ref, ref, loc_d).wait()
 
     def chip_of(d, t):
         return (r + n - t) % n if d == 0 else (r + t) % n
@@ -105,26 +114,24 @@
         return ahead if d == 0 else behind
 
     def hops(which, d):
-        return reach if which == d else n - 1 - reach
+        return n - 1 - reach + jnp.where(which == d, 2 * reach + 1 - n, 0)
 
     def piece(c, p, chip):
         return w_all.at[c, p, block(chip, core), :]
 
     def hop(c, p, d, t):
         ref = piece(c, p, chip_of(d, t - 1))
-        return remote(ref, ref, ring_s.at[c], ring_r.at[c, p, d, t - 1], toward(d))
+        return remote(ref, ref, ring_s, ring_r.at[c % 4, p, d, t - 1], toward(d))
 
     def landed(c, p, d, t):
         ref = piece(c, p, chip_of(d, t))
-        return remote(ref, ref, ring_s.at[c], ring_r.at[c, p, d, t - 1], toward(d))
+        return remote(ref, ref, ring_s, ring_r.at[c % 4, p, d, t - 1], toward(d))
 
     def share(c, p, chip):
         ref = piece(c, p, chip)
-        return remote(ref, ref, peer_s.at[c], peer_r.at[c], peer)
+        return remote(ref, ref, peer_s, peer_r.at[c], peer)
 
     def begin(c):
-        ref = w_all.at[c, :, 0:rows, :]
-        pltpu.make_async_copy(ref, ref, loc_w.at[c]).wait()
         for p in PAIRS:
             for d in DIRS:
                 hop(c, p, d, 1).start()
@@ -133,7 +140,7 @@
 
     def pump(c, t):
         for p, d in ((0, 0), (1, 1), (1, 0), (0, 1)):
-            last = hops(p, d)
+            last = reach if p == d else n - 1 - reach
 
             @pl.when(t <= last)
             def _():
@@ -145,25 +152,20 @@
 
                 share(c, p, chip_of(d, t)).start()
 
-    def dpiece(j, w, chip, c=core):
-        return wd_all.at[j, w, block(chip, c), :]
-
     def dhop(j, d, t):
         ref = dpiece(j, y, chip_of(d, t - 1))
-        return remote(ref, ref, dring_s.at[j], dring_r.at[j, d, t - 1], toward(d))
+        return remote(ref, ref, dring_s, dring_r.at[j % 2, d, t - 1], toward(d))
 
     def dlanded(j, d, t):
         ref = dpiece(j, y, chip_of(d, t))
-        return remote(ref, ref, dring_s.at[j], dring_r.at[j, d, t - 1], toward(d))
+        return remote(ref, ref, dring_s, dring_r.at[j % 2, d, t - 1], toward(d))
 
     def dspread(j, chip):
         ref = dpiece(j, y, chip)
-        remote(ref, ref, dpeer_s.at[j], dpeer_r.at[j], peer).start()
-        remote(ref, ref, dpart_s.at[j], dpart_r.at[j, chip], partner).start()
+        remote(ref, ref, dpeer_s, dpeer_r.at[j], peer).start()
+        remote(ref, ref, dpart_s, dpart_r.at[j], partner).start()
 
     def dbegin(j):
-        ref = wd_all.at[j, y, mine, :]
-        pltpu.make_async_copy(ref, ref, loc_d.at[j]).wait()
         for d in DIRS:
             dhop(j, d, 1).start()
         dspread(j, r)
@@ -172,7 +174,7 @@
         for d in DIRS:
             last = hops(j % 2, d)
 
-            @pl.when((t >= 1) & (t <= last))
+            @pl.when(t <= last)
             def _():
                 dlanded(j, d, t).wait_recv()
 
@@ -182,15 +184,10 @@
 
                 dspread(j, chip_of(d, t))
 
-    def drelay(j, t):
-        for d in DIRS:
-            last = hops(j % 2, d)
-
-            @pl.when((t >= d) & (t <= last))
-            def _():
-                ref = dpiece(j, other, chip_of(d, t))
-                remote(ref, ref, dpart_s.at[j], dpart_r.at[j, chip_of(d, t)], partner).wait_recv()
-                remote(ref, ref, drel_s.at[j], drel_r.at[j], peer).start()
+    def drelay(j):
+        ref = wd_all.at[j, other, :, core]
+        remote(ref, ref, dpart_s, dpart_r.at[j], partner).wait_recv()
+        remote(ref, ref, drel_s, drel_r.at[j], peer).start()
 
     row_id = lax.broadcasted_iota(jnp.int32, (steps, steps), 0)
     lane_id = lax.broadcasted_iota(jnp.int32, (steps, steps), 1)
@@ -222,11 +219,11 @@
 
     def product(c):
         ref = w_all.at[c, :, 0 : n * rows, :]
-        remote(ref, ref, peer_s.at[c], peer_r.at[c], peer).wait_recv()
+        remote(ref, ref, peer_s, peer_r.at[c], peer).wait_recv()
 
         @pl.loop(0, 2)
         def _(p):
-            acc[p] = jnp.dot(feat[...], w_all[c, p], preferred_element_type=jnp.float32)
+            acc[c % 2, p] = jnp.dot(feat[...], w_all[c, p], preferred_element_type=jnp.float32)
 
     lo, hi = slice(0, LANE), slice(LANE, 2 * LANE)
 
@@ -235,9 +232,10 @@
 
     def ends_copy(c, d, source, place):
         ref = ends.at[c, source]
-        return remote(ref, ref, ends_s.at[c, d], ends_r.at[c, d], at(place))
+        return remote(ref, ref, ends_s.at[d - 1], ends_r.at[c, d - 1], at(place))
 
     def scan(c):
+        q = c % 2
         cut = pl.ds(pl.multiple_of(c * LANE, LANE), LANE)
         w = [conv_w[k : k + 1, cut] for k in range(KERNEL)]
         b0, b1 = bias[0:1, cut], bias[1:2, cut]
@@ -246,42 +244,42 @@
         tall = min(64, steps)
 
         def earlier(g, j):
-            rolled = pltpu.roll(acc[0, lines(g, seg - j), hi], 1, 0)
+            rolled = pltpu.roll(acc[q, 0, lines(g, seg - j), hi], 1, 0)
             first = count + g * SUB + SUB - j
-            return jnp.where(row == 0, acc[0, first : first + 1, hi], rolled)
+            return jnp.where(row == 0, acc[q, 0, first : first + 1, hi], rolled)
 
         for g in range(games):
             old = [earlier(g, j) for j in range(KERNEL)[:0:-1]]
             for i in range(steps // tall):
                 first = g * steps + i * tall
                 here = slice(first, first + tall)
-                x0 = acc[0, here, hi]
+                x0 = acc[q, 0, here, hi]
                 conv = w[0] * x0
                 for j in range(1, KERNEL):
                     if i:
-                        xj = acc[0, first - j * SUB : first - j * SUB + tall, hi]
+                        xj = acc[q, 0, first - j * SUB : first - j * SUB + tall, hi]
                     else:
                         xj = jnp.concatenate(old[KERNEL - 1 - j :] + [x0[: tall - j * SUB]], 0)
                     conv += w[j] * xj
-                recur = 0.5 * jnp.tanh(0.5 * (acc[1, here, lo] + b0)) + 0.5
-                inflow = 0.5 * jnp.tanh(0.5 * (acc[1, here, hi] + b1)) + 0.5
+                recur = 0.5 * jnp.tanh(0.5 * (acc[q, 1, here, lo] + b0)) + 0.5
+                inflow = 0.5 * jnp.tanh(0.5 * (acc[q, 1, here, hi] + b1)) + 0.5
                 a = jnp.exp(recur * scale)
                 left = 1.0 - a * a
                 root = left * lax.rsqrt(jnp.maximum(left, 1e-30))
-                acc[0, here, lo] = jax.nn.gelu(acc[0, here, lo])
-                acc[1, here, lo] = a
-                acc[1, here, hi] = root * inflow * conv
+                acc[q, 0, here, lo] = jax.nn.gelu(acc[q, 0, here, lo])
+                acc[q, 1, here, lo] = a
+                acc[q, 1, here, hi] = root * inflow * conv
 
         def step(t, state):
             new = []
             for g in range(games):
                 h, p = state[g]
                 here = lines(g, t)
-                a = acc[1, here, lo]
-                h = a * h + acc[1, here, hi]
+                a = acc[q, 1, here, lo]
+                h = a * h + acc[q, 1, here, hi]
                 p = a * p
-                acc[1, here, lo] = p
-                acc[1, here, hi] = h
+                acc[q, 1, here, lo] = p
+                acc[q, 1, here, hi] = h
                 new.append((h, p))
             return tuple(new)
 
@@ -291,8 +289,8 @@
             h, p = final[g]
             run, dec = jnp.zeros((1, LANE), jnp.float32), jnp.ones((1, LANE), jnp.float32)
             for s in range(SUB):
-                carry_s[g, 0, s : s + 1, :] = run
-                carry_s[g, 1, s : s + 1, :] = dec
+                carry_s[q, g, 0, s : s + 1, :] = run
+                carry_s[q, g, 1, s : s + 1, :] = dec
                 run = p[s : s + 1] * run + h[s : s + 1]
                 dec = p[s : s + 1] * dec
             ends[c, z, 2 * g : 2 * g + 1, :] = run
@@ -304,9 +302,10 @@
                 ends_copy(c, d, z, (z + d, x)).start()
 
     def mix_copy(c):
-        return remote(mix.at[c, other], mix_in.at[c], mix_s.at[c], mix_r.at[c], partner)
+        return remote(mix.at[c, other], mix_in.at[c], mix_s, mix_r.at[c], partner)
 
     def finish(c):
+        q = c % 2
         for d in range(1, zn):
 
             @pl.when(z >= d)
@@ -317,31 +316,33 @@
             run = jnp.zeros((1, LANE), jnp.float32)
             for j in range(zn - 1):
                 run = jnp.where(j < z, ends[c, j, 2 * g + 1 : 2 * g + 2, :] * run + ends[c, j, 2 * g : 2 * g + 1, :], run)
-            enter = carry_s[g, 0] + carry_s[g, 1] * run
+            enter = carry_s[q, g, 0] + carry_s[q, g, 1] * run
             enter = jnp.concatenate([enter, enter], 0)
             for i in range(steps // 16):
                 here = slice(g * steps + i * 16, g * steps + (i + 1) * 16)
-                value = (acc[1, here, hi] + acc[1, here, lo] * enter) * acc[0, here, lo]
+                value = (acc[q, 1, here, hi] + acc[q, 1, here, lo] * enter) * acc[q, 0, here, lo]
                 mix[c, g, i * 16 : (i + 1) * 16, :] = value.astype(jnp.bfloat16)
         mix_copy(c).start()
 
     def project(j):
         for c in (2 * j, 2 * j + 1):
             mix_copy(c).wait_recv()
-        ref = wd_all.at[j, y, 0 : n * rows, :]
-        remote(ref, ref, dpeer_s.at[j], dpeer_r.at[j], peer).wait_recv()
-        remote(ref, ref, drel_s.at[j], drel_r.at[j], peer).wait_recv()
+        ref = wd_all.at[j, y, :, 0]
+        remote(ref, ref, dpeer_s, dpeer_r.at[j], peer).wait_recv()
+        remote(ref, ref, drel_s, drel_r.at[j], peer).wait_recv()
         own = jnp.concatenate([mix[2 * j, y], mix[2 * j + 1, y]], 1)
         theirs = jnp.concatenate([mix_in[2 * j], mix_in[2 * j + 1]], 1)
         part = min(512, half)
+        chips = part // (2 * rows)
 
         @pl.loop(0, depth // part)
         def _(f):
             cut = pl.ds(pl.multiple_of(f * part, part), part)
             total = down[:, cut]
             for left, w in ((own, y), (theirs, other)):
+                right = wd_all[j, w, pl.ds(f * chips, chips)].reshape(part, wide)
                 total += lax.dot_general(
-                    left, wd_all[j, w, cut, :], (((1,), (1,)), ((), ())), preferred_element_type=jnp.float32
+                    left, right, (((1,), (1,)), ((), ())), preferred_element_type=jnp.float32
                 )
             down[:, cut] = total
 
@@ -365,6 +366,7 @@
 
     own_heads.wait()
     quarter = half // 2
+    final = (chunks + 1) * per - 1
 
     def head_rows(w, c):
         return heads.at[w, :, pl.ds(pl.multiple_of(c * quarter, quarter), quarter)]
@@ -374,35 +376,35 @@
 
     swap_heads = remote(head_rows(y, core), head_rows(y, core), head_s, head_r, partner)
     relay_heads = remote(head_rows(other, core), head_rows(other, core), hrel_s, hrel_r, peer)
-    first_d = [per + j * ((chunks - 2) * per - reach) // max(items - 1, 1) for j in range(items)]
-
-    @pl.loop(0, chunks + 4)
+    @pl.loop(0, chunks + 1)
     def _(k):
         @pl.loop(0, per)
         def _(i):
             slot = k * per + i
-            for j in range(items):
-
-                @pl.when(slot == first_d[j])
+
+            @pl.when((i == per - 1) & (k % 2 == 0) & (k < chunks))
+            def _():
+                dbegin(k // 2)
+
+            @pl.when((i == per - 1) & (k < chunks - 2))
+            def _():
+                begin(k + 2)
+
+            @pl.when(k < chunks)
+            def _():
+                pump(k, i + 1)
+
+            @pl.when(k >= 1)
+            def _():
+                pump(k - 1, per + i + 1)
+
+                @pl.when(slot < final)
                 def _():
-                    dbegin(j)
-
-            @pl.when((i == per - 1) & (k < chunks - 2))
-            def _():
-                begin(k + 2)
-
-            @pl.when(k < chunks)
-            def _():
-                pump(k, i + 1)
-
-            @pl.when((k >= 1) & (k <= chunks))
-            def _():
-                pump(k - 1, per + i + 1)
-
-            for j in range(items):
-                t = slot - first_d[j]
-                dpump(j, t)
-                drelay(j, t - 1)
+                    dpump((slot - per) // reach, (slot - per) % reach + 1)
+
+            @pl.when((slot >= 2 * reach) & (slot % reach == 0))
+            def _():
+                drelay(slot // reach - 2)
 
             @pl.when((k == 2) & (i == per - 1))
             def _():
@@ -418,15 +420,39 @@
             def _():
                 project((k - 5) // 2)
 
-            @pl.when(((i == 0) & (k == 3)) | ((i == per - 1) & (k >= 3) & (k < chunks + 2)))
+            @pl.when(((i == 0) & (k == 3)) | ((i == per - 1) & (k >= 3) & (k < chunks)))
             def _():
                 finish(k - 2 - jnp.where(i == 0, 1, 0))
 
-            @pl.when(((i == 0) & (k >= 3) & (k < chunks + 2)) | ((i == per - 1) & (k == 2)))
+            @pl.when(((i == 0) & (k >= 3)) | ((i == per - 1) & (k == 2)))
             def _():
                 product(k - 2)
                 scan(k - 2)
 
+    product(chunks - 1)
+    scan(chunks - 1)
+    dpump(items - 1, reach)
+    finish(chunks - 2)
+    project(items - 2)
+    finish(chunks - 1)
+    drelay(items - 1)
+    ref = w_all.at[:, :, 0 : (n - 1) * rows, :]
+    remote(ref, ref, ring_s, peer_r.at[0], peer).wait_send()
+    ref = w_all.at[:, :, 0 : n * rows, :]
+    remote(ref, ref, peer_s, peer_r.at[0], peer).wait_send()
+    ref = wd_all.at[:, y, 0 : n - 1, 0]
+    remote(ref, ref, dring_s, dpeer_r.at[0], peer).wait_send()
+    ref = wd_all.at[:, y, :, 0]
+    for sem in (dpeer_s, dpart_s, drel_s):
+        remote(ref, ref, sem, dpeer_r.at[0], peer).wait_send()
+    for d in range(1, zn):
+
+        @pl.when(z + d < zn)
+        def _():
+            ref = ends.at[:, z]
+            remote(ref, ref, ends_s.at[d - 1], ends_r.at[0, d - 1], peer).wait_send()
+
+    project(items - 1)
     remote(head_rows(other, 1 - core), head_rows(other, 1 - core), hrel_s, hrel_r, peer).wait_recv()
     ref = wval_all.at[other]
     remote(ref, ref, val_s, val_r, partner).wait_recv()
@@ -462,6 +488,19 @@
     res[y, 1:2, :] = value
     swap_res = remote(res.at[y], res.at[y], res_s, res_r, partner)
     swap_res.start()
+    swap_feat.wait_send()
+    swap_val.wait_send()
+    swap_heads.wait_send()
+    relay_heads.wait_send()
+
+    @pl.when(z < zn - 1)
+    def _():
+        for i in range(2):
+            tail_copy(i).wait_send()
+
+    ref = mix.at[:, other]
+    remote(ref, ref, mix_s, mix_r.at[0], partner).wait_send()
+
     ref = res.at[other]
     remote(ref, ref, res_s, res_r, partner).wait_recv()
     for owner in range(yn):
@@ -469,36 +508,6 @@
         out[games + owner : games + owner + 1, :] = res[owner, 1:2, :]
 
     swap_res.wait_send()
-    swap_feat.wait_send()
-    swap_val.wait_send()
-    swap_heads.wait_send()
-    relay_heads.wait_send()
-
-    @pl.when(z < zn - 1)
-    def _():
-        for i in range(2):
-            tail_copy(i).wait_send()
-
-    @pl.loop(0, chunks)
-    def _(c):
-        ref = w_all.at[c, :, 0 : (n - 1) * rows, :]
-        remote(ref, ref, ring_s.at[c], peer_r.at[c], peer).wait_send()
-        ref = w_all.at[c, :, 0 : n * rows, :]
-        remote(ref, ref, peer_s.at[c], peer_r.at[c], peer).wait_send()
-        mix_copy(c).wait_send()
-        for d in range(1, zn):
-
-            @pl.when(z + d < zn)
-            def _():
-                ends_copy(c, d, z, (z + d, x)).wait_send()
-
-    @pl.loop(0, items)
-    def _(j):
-        ref = wd_all.at[j, y, 0 : (n - 1) * rows, :]
-        remote(ref, ref, dring_s.at[j], dpeer_r.at[j], peer).wait_send()
-        ref = wd_all.at[j, y, 0 : n * rows, :]
-        for sem in (dpeer_s, dpart_s, drel_s):
-            remote(ref, ref, sem.at[j], dpeer_r.at[j], peer).wait_send()
 
 
 def core_block(emb, wb, wd, heads, wval, conv_w, bias, rates, moves, lengths, outcomes):
@@ -523,13 +532,13 @@
         out_shape=jax.ShapeDtypeStruct((2 * games, steps), f32),
         scratch_shapes=[
             pltpu.VMEM((chunks, 2, depth, wide), b16),
-            pltpu.VMEM((items, yn, depth, wide), b16),
+            pltpu.VMEM((items, yn, n, 2, rows, wide), b16),
             pltpu.VMEM((yn, games, steps, half), b16),
             pltpu.VMEM((count + games * SUB, depth), b16),
             pltpu.VMEM((games * SUB, half), b16),
             pltpu.VMEM((yn, games * SUB, half), b16),
-            pltpu.VMEM((2, count + games * SUB, wide), f32),
-            pltpu.VMEM((games, 2, SUB, LANE), f32),
+            pltpu.VMEM((2, 2, count + games * SUB, wide), f32),
+            pltpu.VMEM((2, games, 2, SUB, LANE), f32),
             pltpu.VMEM((chunks, zn, SUB, LANE), f32),
             pltpu.VMEM((chunks, games, steps, LANE), b16),
             pltpu.VMEM((chunks, steps, LANE), b16),
@@ -537,11 +546,10 @@
             pltpu.VMEM((yn, labels, half), b16),
             pltpu.VMEM((yn, half // LANE, LANE), b16),
             pltpu.VMEM((yn, SUB, steps), f32),
-            dma((chunks,)), dma((items,)), dma, dma, dma, dma, dma((2,)), dma((2,)), dma, dma, dma, dma, dma, dma,
-            dma((chunks,)), dma((chunks, 2, 2, reach)), dma((chunks,)), dma((chunks,)),
-            dma((items,)), dma((items, 2, reach)), dma((items,)), dma((items,)),
-            dma((items,)), dma((items, n)), dma((items,)), dma((items,)),
-            dma((chunks, zn)), dma((chunks, zn)), dma((chunks,)), dma((chunks,)), dma, dma,
+            dma, dma, dma, dma, dma, dma, dma((2,)), dma((2,)), dma, dma, dma, dma, dma, dma,
+            dma, dma((4, 2, 2, reach)), dma, dma((chunks,)), dma, dma((2, 2, reach)), dma, dma((items,)),
+            dma, dma((items,)), dma, dma((items,)),
+            dma((zn - 1,)), dma((chunks, zn - 1)), dma, dma((chunks,)), dma, dma,
         ],
         compiler_params=pltpu.CompilerParams(
             collective_id=0, has_side_effects=True, vmem_limit_bytes=56 * 1024 * 1024

time: 135 us -> 128 us (0.948)
  Pallas kernels: 132 us -> 126 us
    pallas_call x1, Pallas kernels: 132 us -> 126 us  [core_block(): pl.pallas_call(core_kernel, in_specs=[hbm] * 4 + [vmem] * 5 + [smem] * 2,...]
where the time goes in v3:
time: 128 us
  Pallas kernels  126 us (98%)
  local copies, waits for them, and re-layouts  1.33 us (1%)
    pallas_call x1, Pallas kernels, core_block(): pl.pallas_call(core_kernel, in_specs=[hbm] * 4 + [vmem] * 5 + [smem] * 2,...  126 us

profile of v3, /device:TPU:0, one launch (start us, length us, event | category | flops | bytes accessed | tf_op | source)
XLA Modules:
  0.0 127.9 jit_solution(13595224803709151881)
XLA Ops:
  0.6 125.9 %shard_map.122 = f32[4,256]{1,0:T(4,128)} custom-call(bf16[2,256,1024]{2,1,0:T(8,128)(2,1)} %emb.1, bf16[4,128,1024]{2,1,0:T(8,128)(2,1)} %wb.1, bf16[128,1024]{1,0:T(8,128)(2,1)} %wd.1, bf16[362,1024]{1,0:T(8,128)(2,1)} %bitcast.3, bf16[8,128]{1,0:T(8,128)(2,1)} %bitcast.5, f32[4,1024]{1,0:T(4,128)} %conv_w.1, f32[2,1024]{1,0:T(2,128)} %bias.1, ...), custom_call_target="tpu_custom_call" | custom-call | flops 8589934592 | bytes 200000000 | tf_op jit(solution)/shard_map/pallas_call | solution.py:528
  126.6 1.3 %fusion = (f32[2,256]{1,0:T(2,128)}, f32[2,256]{1,0:T(2,128)}) fusion(f32[4,256]{1,0:T(4,128)} %shard_map.122), kind=kLoop, calls=%fused_computation | loop fusion | bytes 8192 | tf_op jit(solution)/shard_map/slice | solution.py:581
